TPU v7x, 16 devices: a 4x2x1 block of a 4x4x8 slice. The times are simulated.
16 devices in a mesh: dp: 2 (over y, z), cp: 8 (over x, core).
Axes of the slice: x: 4, y: 2, z: 1, core: 2. Of those that a mesh axis runs over, the one named last changes fastest.
The devices are a block of a 4x4x8 slice.
Arguments:
- x_in: bfloat16 [16, 512, 2048], P('dp', 'cp'), parts along dimension 0
- positions: int32 [1024], P(('dp', 'cp')), parts along dimension 0
- long_factor: float32 [32], replicated
- norm_gain: float32 [2048], replicated
- w_qkv: bfloat16 [2048, 6144], replicated
- w_out: bfloat16 [2048, 2048], replicated
- grad_y: bfloat16 [16, 512, 2048], P('dp', 'cp'), parts along dimension 0
Outputs:
- output 1: bfloat16 [16, 512, 2048], P('dp', 'cp'), parts along dimension 0
- output 2: bfloat16 [16, 512, 2048], P('dp', 'cp'), parts along dimension 0
- output 3: float32 [4096], P('dp'), parts along dimension 0
- output 4: float32 [4096, 6144], P('dp'), parts along dimension 0
- output 5: float32 [4096, 2048], P('dp'), parts along dimension 0
There are 2 independent parts. A program takes and returns all parts, laid end to end along the dimension named above; an argument that names none is the same for every part.
All inputs are finite; a program needn't handle non-finite values.
Results may differ from a plain program's by a relative error of at most 0.0147614.
Values are sent between devices in bfloat16 or wider.
A program may use at most 768 MiB of HBM per device.

v0:
```python
import math
import jax
import jax.numpy as jnp
from jax import lax
from jax.sharding import PartitionSpec as P

NORM_EPS = 1e-5
MSCALE = math.sqrt(1.0 + math.log(32.0) / math.log(4096.0))
MASK_VALUE = -1e30


def rope_tables(positions, long_factor):
    half = long_factor.shape[0]
    exponent = jnp.arange(half, dtype=jnp.float32) * (1.0 / half)
    inv_freq = 1.0 / (long_factor * jnp.power(10000.0, exponent))
    angles = positions.astype(jnp.float32)[:, None] * inv_freq[None, :]
    angle_pair = jnp.concatenate([angles, angles], axis=-1)
    return (jnp.cos(angle_pair) * MSCALE)[None, :, None, :], (jnp.sin(angle_pair) * MSCALE)[None, :, None, :]


def rotate_half(values):
    half = values.shape[-1] // 2
    return jnp.concatenate([-values[..., half:], values[..., :half]], axis=-1)


def masked_scores(q_blk, k_blk, q_start, k_start, scale):
    scores = jnp.einsum('bqhd,bkhd->bhqk', q_blk, k_blk, preferred_element_type=jnp.float32) * scale
    q_pos = q_start + jnp.arange(q_blk.shape[1])[:, None]
    k_pos = k_start + jnp.arange(k_blk.shape[1])[None, :]
    return jnp.where(k_pos <= q_pos, scores, MASK_VALUE)


def fwd_block(stats, q_blk, k_blk, v_blk, q_start, k_start, scale):
    out_acc, row_max, row_sum = stats
    scores = masked_scores(q_blk, k_blk, q_start, k_start, scale)
    new_max = jnp.maximum(row_max, jnp.max(scores, axis=-1, keepdims=True))
    rescale = jnp.exp(row_max - new_max)
    attn_probs = jnp.exp(scores - new_max)
    row_sum = row_sum * rescale + jnp.sum(attn_probs, axis=-1, keepdims=True)
    pv_part = jnp.einsum('bhqk,bkhd->bqhd', attn_probs.astype(jnp.bfloat16), v_blk, preferred_element_type=jnp.float32)
    out_acc = out_acc * jnp.transpose(rescale, (0, 2, 1, 3)) + pv_part
    return out_acc, new_max, row_sum


def bwd_block(q_blk, k_blk, v_blk, d_attn, log_norm, delta, q_start, k_start, scale):
    attn_probs = jnp.exp(masked_scores(q_blk, k_blk, q_start, k_start, scale) - log_norm)
    dv_part = jnp.einsum('bhqk,bqhd->bkhd', attn_probs.astype(jnp.bfloat16), d_attn, preferred_element_type=jnp.float32)
    d_probs = jnp.einsum('bqhd,bkhd->bhqk', d_attn, v_blk, preferred_element_type=jnp.float32)
    d_scores = (attn_probs * (d_probs - delta) * scale).astype(jnp.bfloat16)
    dq_part = jnp.einsum('bhqk,bkhd->bqhd', d_scores, k_blk, preferred_element_type=jnp.float32)
    dk_part = jnp.einsum('bhqk,bqhd->bkhd', d_scores, q_blk, preferred_element_type=jnp.float32)
    return dq_part, dk_part, dv_part


def solution(mesh):
    cp_size = mesh.shape['cp']
    shift_perm = [(src_dev, (src_dev + 1) % cp_size) for src_dev in range(cp_size)]

    def device_fn(x_in, positions, long_factor, norm_gain, w_qkv, w_out, grad_y):
        batch, piece, hidden = x_in.shape
        head_dim = 2 * long_factor.shape[0]
        width = w_out.shape[0]
        heads = width // head_dim
        scale = 1.0 / math.sqrt(head_dim)
        my_index = lax.axis_index('cp')
        q_start = my_index * piece
        x_float = x_in.astype(jnp.float32)
        inv_rms = lax.rsqrt(jnp.mean(x_float * x_float, axis=-1, keepdims=True) + NORM_EPS)
        x_hat = x_float * inv_rms
        normed = (x_hat * norm_gain).astype(jnp.bfloat16)
        qkv_proj = jnp.einsum('bsd,de->bse', normed, w_qkv, preferred_element_type=jnp.float32)
        qkv_proj = qkv_proj.reshape(batch, piece, 3, heads, head_dim)
        cos_tab, sin_tab = rope_tables(positions, long_factor)
        q_rot = (qkv_proj[:, :, 0] * cos_tab + rotate_half(qkv_proj[:, :, 0]) * sin_tab).astype(jnp.bfloat16)
        k_rot = (qkv_proj[:, :, 1] * cos_tab + rotate_half(qkv_proj[:, :, 1]) * sin_tab).astype(jnp.bfloat16)
        v_val = qkv_proj[:, :, 2].astype(jnp.bfloat16)

        init_stats = (jnp.zeros((batch, piece, heads, head_dim), jnp.float32), jnp.full((batch, heads, piece, 1), MASK_VALUE, jnp.float32), jnp.zeros((batch, heads, piece, 1), jnp.float32))
        stats = fwd_block(init_stats, q_rot, k_rot, v_val, q_start, q_start, scale)

        def fwd_step(step_idx, state):
            stats, k_cur, v_cur = state
            k_cur = lax.ppermute(k_cur, 'cp', shift_perm)
            v_cur = lax.ppermute(v_cur, 'cp', shift_perm)
            k_start = (my_index - step_idx) * piece
            stats = lax.cond(step_idx <= my_index, lambda acc: fwd_block(acc, q_rot, k_cur, v_cur, q_start, k_start, scale), lambda acc: acc, stats)
            return stats, k_cur, v_cur

        stats, _, _ = lax.fori_loop(1, cp_size, fwd_step, (stats, k_rot, v_val))
        out_acc, row_max, row_sum = stats
        attn_out = (out_acc / jnp.transpose(row_sum, (0, 2, 1, 3))).astype(jnp.bfloat16)
        log_norm = row_max + jnp.log(row_sum)
        attn_flat = attn_out.reshape(batch, piece, width)
        y_out = (x_float + jnp.einsum('bsh,hd->bsd', attn_flat, w_out, preferred_element_type=jnp.float32)).astype(jnp.bfloat16)

        d_attn = jnp.einsum('bsd,hd->bsh', grad_y, w_out, preferred_element_type=jnp.float32).astype(jnp.bfloat16).reshape(batch, piece, heads, head_dim)
        g_wout = jnp.einsum('bsh,bsd->hd', attn_flat, grad_y, preferred_element_type=jnp.float32)
        delta = jnp.einsum('bqhd,bqhd->bhq', d_attn, attn_out, preferred_element_type=jnp.float32)[..., None]
        dq_acc, dk_own, dv_own = bwd_block(q_rot, k_rot, v_val, d_attn, log_norm, delta, q_start, q_start, scale)

        def bwd_step(step_idx, state):
            dq_acc, k_cur, v_cur, dk_cur, dv_cur = state
            k_cur = lax.ppermute(k_cur, 'cp', shift_perm)
            v_cur = lax.ppermute(v_cur, 'cp', shift_perm)
            dk_cur = lax.ppermute(dk_cur, 'cp', shift_perm)
            dv_cur = lax.ppermute(dv_cur, 'cp', shift_perm)
            k_start = (my_index - step_idx) * piece

            def add_block(sums):
                dq_sum, dk_sum, dv_sum = sums
                dq_part, dk_part, dv_part = bwd_block(q_rot, k_cur, v_cur, d_attn, log_norm, delta, q_start, k_start, scale)
                return dq_sum + dq_part, dk_sum + dk_part, dv_sum + dv_part

            dq_acc, dk_cur, dv_cur = lax.cond(step_idx <= my_index, add_block, lambda sums: sums, (dq_acc, dk_cur, dv_cur))
            return dq_acc, k_cur, v_cur, dk_cur, dv_cur

        dq_acc, _, _, dk_cur, dv_cur = lax.fori_loop(1, cp_size, bwd_step, (dq_acc, k_rot, v_val, dk_own, dv_own))
        dk_home = lax.ppermute(dk_cur, 'cp', shift_perm)
        dv_home = lax.ppermute(dv_cur, 'cp', shift_perm)

        dq_raw = dq_acc * cos_tab - rotate_half(dq_acc * sin_tab)
        dk_raw = dk_home * cos_tab - rotate_half(dk_home * sin_tab)
        d_qkv = jnp.stack([dq_raw.astype(jnp.bfloat16), dk_raw.astype(jnp.bfloat16), dv_home.astype(jnp.bfloat16)], axis=2).reshape(batch, piece, 3 * width)
        g_wqkv = jnp.einsum('bsd,bse->de', normed, d_qkv, preferred_element_type=jnp.float32)
        d_normed = jnp.einsum('bse,de->bsd', d_qkv, w_qkv, preferred_element_type=jnp.float32)
        g_gain = jnp.sum(d_normed * x_hat, axis=(0, 1))
        d_hat = d_normed * norm_gain
        dx_norm = inv_rms * (d_hat - x_hat * jnp.mean(d_hat * x_hat, axis=-1, keepdims=True))
        grad_x = (grad_y.astype(jnp.float32) + dx_norm).astype(jnp.bfloat16)
        g_gain, g_wqkv, g_wout = lax.psum((g_gain, g_wqkv, g_wout), 'cp')
        return y_out, grad_x, g_gain, g_wqkv, g_wout

    seq_spec = P('dp', 'cp', None)
    return jax.shard_map(device_fn, mesh=mesh, in_specs=(seq_spec, P(('dp', 'cp')), P(None), P(None), P(None, None), P(None, None), seq_spec), out_specs=(seq_spec, seq_spec, P('dp'), P('dp', None), P('dp', None)), check_vma=False)
```

profile of v0, /device:TPU:112, one launch (start us, length us, event | category | flops | bytes accessed | tf_op | source)
XLA Modules:
  0.0 4336.6 jit_solution(16773915815649793219)
XLA Ops:
  194.4 830.3 %while.42 = (s32[]{:T(128)}, f32[8,64,32,64]{3,1,2,0:T(8,128)}, f32[8,32,64,1]{2,1,0,3:T(8,128)S(1)}, f32[8,32,64,1]{2,1,0,3:T(8,128)S(1)}, bf16[8,64,32,64]{3,1...) while((s32[]{:T(128)}, f32[8,64,32,64]{3,1,2,0:T(8,128)}, ...), condition=%wide.region_8.9_spmd, body=%wide.region_3.8_spmd.sunk | while | flops 282120320 | bytes 95438256 | solution.py:89
  196.8 47.1 %collective-permute-done.1 = bf16[8,64,32,64]{3,1,2,0:T(8,128)(2,1)} collective-permute-done((bf16[8,64,32,64]{3,1,2,0:T(8,128)(2,1)}, bf16[8,64,32,64]{3,1,2,0:T(8,128)(2,1)}, u32[]{:S(2)}, u32[]{:S(2)}) %collective-permute-start.1) | collective-permute-done | bytes 2097184 | tf_op jit(solution)/shard_map/while/body/eval_jaxpr/ppermute | solution.py:84
  243.9 44.9 %collective-permute-done = bf16[8,64,32,64]{3,1,2,0:T(8,128)(2,1)} collective-permute-done((bf16[8,64,32,64]{3,1,2,0:T(8,128)(2,1)}, bf16[8,64,32,64]{3,1,2,0:T(8,128)(2,1)}, u32[]{:S(2)}, u32[]{:S(2)}) %collective-permute-start) | collective-permute-done | bytes 2097184 | tf_op jit(solution)/shard_map/while/body/eval_jaxpr/ppermute | solution.py:83
  320.2 44.6 %collective-permute-done.1 = bf16[8,64,32,64]{3,1,2,0:T(8,128)(2,1)} collective-permute-done((bf16[8,64,32,64]{3,1,2,0:T(8,128)(2,1)}, bf16[8,64,32,64]{3,1,2,0:T(8,128)(2,1)}, u32[]{:S(2)}, u32[]{:S(2)}) %collective-permute-start.1) | collective-permute-done | bytes 2097184 | tf_op jit(solution)/shard_map/while/body/eval_jaxpr/ppermute | solution.py:84
  364.8 44.9 %collective-permute-done = bf16[8,64,32,64]{3,1,2,0:T(8,128)(2,1)} collective-permute-done((bf16[8,64,32,64]{3,1,2,0:T(8,128)(2,1)}, bf16[8,64,32,64]{3,1,2,0:T(8,128)(2,1)}, u32[]{:S(2)}, u32[]{:S(2)}) %collective-permute-start) | collective-permute-done | bytes 2097184 | tf_op jit(solution)/shard_map/while/body/eval_jaxpr/ppermute | solution.py:83
  443.6 42.1 collective-permute-done.1
  485.7 44.9 %collective-permute-done = bf16[8,64,32,64]{3,1,2,0:T(8,128)(2,1)} collective-permute-done((bf16[8,64,32,64]{3,1,2,0:T(8,128)(2,1)}, bf16[8,64,32,64]{3,1,2,0:T(8,128)(2,1)}, u32[]{:S(2)}, u32[]{:S(2)}) %collective-permute-start) | collective-permute-done | bytes 2097184 | tf_op jit(solution)/shard_map/while/body/eval_jaxpr/ppermute | solution.py:83
  546.9 59.7 %collective-permute-done.1 = bf16[8,64,32,64]{3,1,2,0:T(8,128)(2,1)} collective-permute-done((bf16[8,64,32,64]{3,1,2,0:T(8,128)(2,1)}, bf16[8,64,32,64]{3,1,2,0:T(8,128)(2,1)}, u32[]{:S(2)}, u32[]{:S(2)}) %collective-permute-start.1) | collective-permute-done | bytes 2097184 | tf_op jit(solution)/shard_map/while/body/eval_jaxpr/ppermute | solution.py:84
  606.6 44.9 %collective-permute-done = bf16[8,64,32,64]{3,1,2,0:T(8,128)(2,1)} collective-permute-done((bf16[8,64,32,64]{3,1,2,0:T(8,128)(2,1)}, bf16[8,64,32,64]{3,1,2,0:T(8,128)(2,1)}, u32[]{:S(2)}, u32[]{:S(2)}) %collective-permute-start) | collective-permute-done | bytes 2097184 | tf_op jit(solution)/shard_map/while/body/eval_jaxpr/ppermute | solution.py:83
  662.0 65.5 %collective-permute-done.1 = bf16[8,64,32,64]{3,1,2,0:T(8,128)(2,1)} collective-permute-done((bf16[8,64,32,64]{3,1,2,0:T(8,128)(2,1)}, bf16[8,64,32,64]{3,1,2,0:T(8,128)(2,1)}, u32[]{:S(2)}, u32[]{:S(2)}) %collective-permute-start.1) | collective-permute-done | bytes 2097184 | tf_op jit(solution)/shard_map/while/body/eval_jaxpr/ppermute | solution.py:84
  727.5 44.9 %collective-permute-done = bf16[8,64,32,64]{3,1,2,0:T(8,128)(2,1)} collective-permute-done((bf16[8,64,32,64]{3,1,2,0:T(8,128)(2,1)}, bf16[8,64,32,64]{3,1,2,0:T(8,128)(2,1)}, u32[]{:S(2)}, u32[]{:S(2)}) %collective-permute-start) | collective-permute-done | bytes 2097184 | tf_op jit(solution)/shard_map/while/body/eval_jaxpr/ppermute | solution.py:83
  782.9 65.5 %collective-permute-done.1 = bf16[8,64,32,64]{3,1,2,0:T(8,128)(2,1)} collective-permute-done((bf16[8,64,32,64]{3,1,2,0:T(8,128)(2,1)}, bf16[8,64,32,64]{3,1,2,0:T(8,128)(2,1)}, u32[]{:S(2)}, u32[]{:S(2)}) %collective-permute-start.1) | collective-permute-done | bytes 2097184 | tf_op jit(solution)/shard_map/while/body/eval_jaxpr/ppermute | solution.py:84
  848.4 44.9 %collective-permute-done = bf16[8,64,32,64]{3,1,2,0:T(8,128)(2,1)} collective-permute-done((bf16[8,64,32,64]{3,1,2,0:T(8,128)(2,1)}, bf16[8,64,32,64]{3,1,2,0:T(8,128)(2,1)}, u32[]{:S(2)}, u32[]{:S(2)}) %collective-permute-start) | collective-permute-done | bytes 2097184 | tf_op jit(solution)/shard_map/while/body/eval_jaxpr/ppermute | solution.py:83
  903.8 65.5 %collective-permute-done.1 = bf16[8,64,32,64]{3,1,2,0:T(8,128)(2,1)} collective-permute-done((bf16[8,64,32,64]{3,1,2,0:T(8,128)(2,1)}, bf16[8,64,32,64]{3,1,2,0:T(8,128)(2,1)}, u32[]{:S(2)}, u32[]{:S(2)}) %collective-permute-start.1) | collective-permute-done | bytes 2097184 | tf_op jit(solution)/shard_map/while/body/eval_jaxpr/ppermute | solution.py:84
  969.2 44.9 %collective-permute-done = bf16[8,64,32,64]{3,1,2,0:T(8,128)(2,1)} collective-permute-done((bf16[8,64,32,64]{3,1,2,0:T(8,128)(2,1)}, bf16[8,64,32,64]{3,1,2,0:T(8,128)(2,1)}, u32[]{:S(2)}, u32[]{:S(2)}) %collective-permute-start) | collective-permute-done | bytes 2097184 | tf_op jit(solution)/shard_map/while/body/eval_jaxpr/ppermute | solution.py:83
  1101.0 2302.4 %while.43 = (s32[]{:T(128)}, f32[8,64,32,64]{3,1,2,0:T(8,128)}, bf16[8,64,32,64]{3,1,2,0:T(8,128)(2,1)}, bf16[8,64,32,64]{3,1,2,0:T(8,128)(2,1)}, f32[8,64,32,64...) while((s32[]{:T(128)}, f32[8,64,32,64]{3,1,2,0:T(8,128)}, ...), condition=%wide.region_12.13_spmd, body=%wide.region_9.12_spmd.sunk | while | flops 685772928 | bytes 151205392 | solution.py:117
  1101.5 245.0 %collective-permute-done.5 = bf16[8,64,32,64]{3,1,2,0:T(8,128)(2,1)} collective-permute-done((bf16[8,64,32,64]{3,1,2,0:T(8,128)(2,1)}, bf16[8,64,32,64]{3,1,2,0:T(8,128)(2,1)}, u32[]{:S(2)}, u32[]{:S(2)}) %collective-permute-start.5) | collective-permute-done | bytes 2097184 | tf_op jit(solution)/shard_map/while/body/eval_jaxpr/ppermute | solution.py:104
  1351.8 39.7 collective-permute-done.4
  1413.4 264.7 %collective-permute-done.5 = bf16[8,64,32,64]{3,1,2,0:T(8,128)(2,1)} collective-permute-done((bf16[8,64,32,64]{3,1,2,0:T(8,128)(2,1)}, bf16[8,64,32,64]{3,1,2,0:T(8,128)(2,1)}, u32[]{:S(2)}, u32[]{:S(2)}) %collective-permute-start.5) | collective-permute-done | bytes 2097184 | tf_op jit(solution)/shard_map/while/body/eval_jaxpr/ppermute | solution.py:104
  1683.4 39.7 collective-permute-done.4
  1747.0 262.7 %collective-permute-done.5 = bf16[8,64,32,64]{3,1,2,0:T(8,128)(2,1)} collective-permute-done((bf16[8,64,32,64]{3,1,2,0:T(8,128)(2,1)}, bf16[8,64,32,64]{3,1,2,0:T(8,128)(2,1)}, u32[]{:S(2)}, u32[]{:S(2)}) %collective-permute-start.5) | collective-permute-done | bytes 2097184 | tf_op jit(solution)/shard_map/while/body/eval_jaxpr/ppermute | solution.py:104
  2015.0 39.7 collective-permute-done.4
  2081.1 260.2 %collective-permute-done.5 = bf16[8,64,32,64]{3,1,2,0:T(8,128)(2,1)} collective-permute-done((bf16[8,64,32,64]{3,1,2,0:T(8,128)(2,1)}, bf16[8,64,32,64]{3,1,2,0:T(8,128)(2,1)}, u32[]{:S(2)}, u32[]{:S(2)}) %collective-permute-start.5) | collective-permute-done | bytes 2097184 | tf_op jit(solution)/shard_map/while/body/eval_jaxpr/ppermute | solution.py:104
  2346.6 39.7 collective-permute-done.4
  2415.2 257.7 %collective-permute-done.5 = bf16[8,64,32,64]{3,1,2,0:T(8,128)(2,1)} collective-permute-done((bf16[8,64,32,64]{3,1,2,0:T(8,128)(2,1)}, bf16[8,64,32,64]{3,1,2,0:T(8,128)(2,1)}, u32[]{:S(2)}, u32[]{:S(2)}) %collective-permute-start.5) | collective-permute-done | bytes 2097184 | tf_op jit(solution)/shard_map/while/body/eval_jaxpr/ppermute | solution.py:104
  2678.3 39.7 collective-permute-done.4
  2739.9 264.7 %collective-permute-done.5 = bf16[8,64,32,64]{3,1,2,0:T(8,128)(2,1)} collective-permute-done((bf16[8,64,32,64]{3,1,2,0:T(8,128)(2,1)}, bf16[8,64,32,64]{3,1,2,0:T(8,128)(2,1)}, u32[]{:S(2)}, u32[]{:S(2)}) %collective-permute-start.5) | collective-permute-done | bytes 2097184 | tf_op jit(solution)/shard_map/while/body/eval_jaxpr/ppermute | solution.py:104
  3009.9 39.7 collective-permute-done.4
  3071.5 264.7 %collective-permute-done.5 = bf16[8,64,32,64]{3,1,2,0:T(8,128)(2,1)} collective-permute-done((bf16[8,64,32,64]{3,1,2,0:T(8,128)(2,1)}, bf16[8,64,32,64]{3,1,2,0:T(8,128)(2,1)}, u32[]{:S(2)}, u32[]{:S(2)}) %collective-permute-start.5) | collective-permute-done | bytes 2097184 | tf_op jit(solution)/shard_map/while/body/eval_jaxpr/ppermute | solution.py:104
  3341.5 39.7 collective-permute-done.4
  3431.9 101.6 %collective-permute-done.6 = f32[8,64,32,64]{3,1,2,0:T(8,128)} collective-permute-done((f32[8,64,32,64]{3,1,2,0:T(8,128)}, f32[8,64,32,64]{3,1,2,0:T(8,128)}, u32[]{:S(2)}, u32[]{:S(2)}) %collective-permute-start.6) | collective-permute-done | bytes 4194336 | tf_op jit(solution)/shard_map/ppermute | solution.py:118
  3683.7 599.4 %all-reduce.3.cloned.1.call-done = (f32[2048,6144]{1,0:T(8,128)}, f32[2048,2048]{1,0:T(8,128)}) async-done(((f32[2048,6144]{1,0:T(8,128)}, f32[2048,2048]{1,0:T(8,128)}), (f32[2048,6144]{1,0:T(8,128)}, f32[2048,2048]{1,0:T(8,128)})) %all-reduce.3.cloned.1.call-update) | async-done | bytes 67108880 | tf_op jit(solution)/shard_map/psum | solution.py:130
  (229 shorter events, 818.3 us)
Async XLA Ops:
  7.2 4276.0 %all-reduce.3.cloned.1.call-start = ((), (), s32[]{:S(2)}) async-start(), calls=%async_computation | async-start | bytes 134217728 | tf_op jit(solution)/shard_map/psum | solution.py:130
  662.0 110.4 %collective-permute-start = (bf16[8,64,32,64]{3,1,2,0:T(8,128)(2,1)}, bf16[8,64,32,64]{3,1,2,0:T(8,128)(2,1)}, u32[]{:S(2)}, u32[]{:S(2)}) collective-permute-start(bf16[8,64,32,64]{3,1,2,0:T(8,128)(2,1)} %get-tuple-element.800), channel_id=1, source_target_pairs={{0,1},{1,2},{2,3},{3,4},{4,5},{5,6},{6,7},{7,0},{8,9},{9,10},{10,1... | collective-permute-start | bytes 6291464 | tf_op jit(solution)/shard_map/while/body/eval_jaxpr/ppermute | solution.py:83
  1101.2 295.5 %collective-permute-start.3 = (f32[8,64,32,64]{3,1,2,0:T(8,128)}, f32[8,64,32,64]{3,1,2,0:T(8,128)}, u32[]{:S(2)}, u32[]{:S(2)}) collective-permute-start(f32[8,64,32,64]{3,1,2,0:T(8,128)} %get-tuple-element.834), channel_id=1, source_target_pairs={{0,1},{1,2},{2,3},{3,4},{4,5},{5,6},{6,7},{7,0},{8,9},{9,10},{10,1... | collective-permute-start | bytes 12582920 | tf_op jit(solution)/shard_map/while/body/eval_jaxpr/ppermute | solution.py:106
  1101.3 295.4 %collective-permute-start.2 = (f32[8,64,32,64]{3,1,2,0:T(8,128)}, f32[8,64,32,64]{3,1,2,0:T(8,128)}, u32[]{:S(2)}, u32[]{:S(2)}) collective-permute-start(f32[8,64,32,64]{3,1,2,0:T(8,128)} %get-tuple-element.833), channel_id=1, source_target_pairs={{0,1},{1,2},{2,3},{3,4},{4,5},{5,6},{6,7},{7,0},{8,9},{9,10},{10,1... | collective-permute-start | bytes 12582920 | tf_op jit(solution)/shard_map/while/body/eval_jaxpr/ppermute | solution.py:105
  1101.3 245.1 %collective-permute-start.5 = (bf16[8,64,32,64]{3,1,2,0:T(8,128)(2,1)}, bf16[8,64,32,64]{3,1,2,0:T(8,128)(2,1)}, u32[]{:S(2)}, u32[]{:S(2)}) collective-permute-start(bf16[8,64,32,64]{3,1,2,0:T(8,128)(2,1)} %get-tuple-element.832), channel_id=1, source_target_pairs={{0,1},{1,2},{2,3},{3,4},{4,5},{5,6},{6,7},{7,0},{8,9},{9,10},{10,1... | collective-permute-start | bytes 6291464 | tf_op jit(solution)/shard_map/while/body/eval_jaxpr/ppermute | solution.py:104
  1101.4 290.0 %collective-permute-start.4 = (bf16[8,64,32,64]{3,1,2,0:T(8,128)(2,1)}, bf16[8,64,32,64]{3,1,2,0:T(8,128)(2,1)}, u32[]{:S(2)}, u32[]{:S(2)}) collective-permute-start(bf16[8,64,32,64]{3,1,2,0:T(8,128)(2,1)} %get-tuple-element.831), channel_id=1, source_target_pairs={{0,1},{1,2},{2,3},{3,4},{4,5},{5,6},{6,7},{7,0},{8,9},{9,10},{10,1... | collective-permute-start | bytes 6291464 | tf_op jit(solution)/shard_map/while/body/eval_jaxpr/ppermute | solution.py:103
  1413.3 315.0 %collective-permute-start.3 = (f32[8,64,32,64]{3,1,2,0:T(8,128)}, f32[8,64,32,64]{3,1,2,0:T(8,128)}, u32[]{:S(2)}, u32[]{:S(2)}) collective-permute-start(f32[8,64,32,64]{3,1,2,0:T(8,128)} %get-tuple-element.834), channel_id=1, source_target_pairs={{0,1},{1,2},{2,3},{3,4},{4,5},{5,6},{6,7},{7,0},{8,9},{9,10},{10,1... | collective-permute-start | bytes 12582920 | tf_op jit(solution)/shard_map/while/body/eval_jaxpr/ppermute | solution.py:106
  1413.3 315.0 %collective-permute-start.2 = (f32[8,64,32,64]{3,1,2,0:T(8,128)}, f32[8,64,32,64]{3,1,2,0:T(8,128)}, u32[]{:S(2)}, u32[]{:S(2)}) collective-permute-start(f32[8,64,32,64]{3,1,2,0:T(8,128)} %get-tuple-element.833), channel_id=1, source_target_pairs={{0,1},{1,2},{2,3},{3,4},{4,5},{5,6},{6,7},{7,0},{8,9},{9,10},{10,1... | collective-permute-start | bytes 12582920 | tf_op jit(solution)/shard_map/while/body/eval_jaxpr/ppermute | solution.py:105
  1413.3 264.8 %collective-permute-start.5 = (bf16[8,64,32,64]{3,1,2,0:T(8,128)(2,1)}, bf16[8,64,32,64]{3,1,2,0:T(8,128)(2,1)}, u32[]{:S(2)}, u32[]{:S(2)}) collective-permute-start(bf16[8,64,32,64]{3,1,2,0:T(8,128)(2,1)} %get-tuple-element.832), channel_id=1, source_target_pairs={{0,1},{1,2},{2,3},{3,4},{4,5},{5,6},{6,7},{7,0},{8,9},{9,10},{10,1... | collective-permute-start | bytes 6291464 | tf_op jit(solution)/shard_map/while/body/eval_jaxpr/ppermute | solution.py:104
  1413.3 309.7 %collective-permute-start.4 = (bf16[8,64,32,64]{3,1,2,0:T(8,128)(2,1)}, bf16[8,64,32,64]{3,1,2,0:T(8,128)(2,1)}, u32[]{:S(2)}, u32[]{:S(2)}) collective-permute-start(bf16[8,64,32,64]{3,1,2,0:T(8,128)(2,1)} %get-tuple-element.831), channel_id=1, source_target_pairs={{0,1},{1,2},{2,3},{3,4},{4,5},{5,6},{6,7},{7,0},{8,9},{9,10},{10,1... | collective-permute-start | bytes 6291464 | tf_op jit(solution)/shard_map/while/body/eval_jaxpr/ppermute | solution.py:103
  1744.9 315.0 %collective-permute-start.3 = (f32[8,64,32,64]{3,1,2,0:T(8,128)}, f32[8,64,32,64]{3,1,2,0:T(8,128)}, u32[]{:S(2)}, u32[]{:S(2)}) collective-permute-start(f32[8,64,32,64]{3,1,2,0:T(8,128)} %get-tuple-element.834), channel_id=1, source_target_pairs={{0,1},{1,2},{2,3},{3,4},{4,5},{5,6},{6,7},{7,0},{8,9},{9,10},{10,1... | collective-permute-start | bytes 12582920 | tf_op jit(solution)/shard_map/while/body/eval_jaxpr/ppermute | solution.py:106
  1744.9 315.0 %collective-permute-start.2 = (f32[8,64,32,64]{3,1,2,0:T(8,128)}, f32[8,64,32,64]{3,1,2,0:T(8,128)}, u32[]{:S(2)}, u32[]{:S(2)}) collective-permute-start(f32[8,64,32,64]{3,1,2,0:T(8,128)} %get-tuple-element.833), channel_id=1, source_target_pairs={{0,1},{1,2},{2,3},{3,4},{4,5},{5,6},{6,7},{7,0},{8,9},{9,10},{10,1... | collective-permute-start | bytes 12582920 | tf_op jit(solution)/shard_map/while/body/eval_jaxpr/ppermute | solution.py:105
  1744.9 264.8 %collective-permute-start.5 = (bf16[8,64,32,64]{3,1,2,0:T(8,128)(2,1)}, bf16[8,64,32,64]{3,1,2,0:T(8,128)(2,1)}, u32[]{:S(2)}, u32[]{:S(2)}) collective-permute-start(bf16[8,64,32,64]{3,1,2,0:T(8,128)(2,1)} %get-tuple-element.832), channel_id=1, source_target_pairs={{0,1},{1,2},{2,3},{3,4},{4,5},{5,6},{6,7},{7,0},{8,9},{9,10},{10,1... | collective-permute-start | bytes 6291464 | tf_op jit(solution)/shard_map/while/body/eval_jaxpr/ppermute | solution.py:104
  1744.9 309.7 %collective-permute-start.4 = (bf16[8,64,32,64]{3,1,2,0:T(8,128)(2,1)}, bf16[8,64,32,64]{3,1,2,0:T(8,128)(2,1)}, u32[]{:S(2)}, u32[]{:S(2)}) collective-permute-start(bf16[8,64,32,64]{3,1,2,0:T(8,128)(2,1)} %get-tuple-element.831), channel_id=1, source_target_pairs={{0,1},{1,2},{2,3},{3,4},{4,5},{5,6},{6,7},{7,0},{8,9},{9,10},{10,1... | collective-permute-start | bytes 6291464 | tf_op jit(solution)/shard_map/while/body/eval_jaxpr/ppermute | solution.py:103
  2076.5 315.0 %collective-permute-start.3 = (f32[8,64,32,64]{3,1,2,0:T(8,128)}, f32[8,64,32,64]{3,1,2,0:T(8,128)}, u32[]{:S(2)}, u32[]{:S(2)}) collective-permute-start(f32[8,64,32,64]{3,1,2,0:T(8,128)} %get-tuple-element.834), channel_id=1, source_target_pairs={{0,1},{1,2},{2,3},{3,4},{4,5},{5,6},{6,7},{7,0},{8,9},{9,10},{10,1... | collective-permute-start | bytes 12582920 | tf_op jit(solution)/shard_map/while/body/eval_jaxpr/ppermute | solution.py:106
  2076.5 315.0 %collective-permute-start.2 = (f32[8,64,32,64]{3,1,2,0:T(8,128)}, f32[8,64,32,64]{3,1,2,0:T(8,128)}, u32[]{:S(2)}, u32[]{:S(2)}) collective-permute-start(f32[8,64,32,64]{3,1,2,0:T(8,128)} %get-tuple-element.833), channel_id=1, source_target_pairs={{0,1},{1,2},{2,3},{3,4},{4,5},{5,6},{6,7},{7,0},{8,9},{9,10},{10,1... | collective-permute-start | bytes 12582920 | tf_op jit(solution)/shard_map/while/body/eval_jaxpr/ppermute | solution.py:105
  2076.5 264.8 %collective-permute-start.5 = (bf16[8,64,32,64]{3,1,2,0:T(8,128)(2,1)}, bf16[8,64,32,64]{3,1,2,0:T(8,128)(2,1)}, u32[]{:S(2)}, u32[]{:S(2)}) collective-permute-start(bf16[8,64,32,64]{3,1,2,0:T(8,128)(2,1)} %get-tuple-element.832), channel_id=1, source_target_pairs={{0,1},{1,2},{2,3},{3,4},{4,5},{5,6},{6,7},{7,0},{8,9},{9,10},{10,1... | collective-permute-start | bytes 6291464 | tf_op jit(solution)/shard_map/while/body/eval_jaxpr/ppermute | solution.py:104
  2078.6 307.7 %collective-permute-start.4 = (bf16[8,64,32,64]{3,1,2,0:T(8,128)(2,1)}, bf16[8,64,32,64]{3,1,2,0:T(8,128)(2,1)}, u32[]{:S(2)}, u32[]{:S(2)}) collective-permute-start(bf16[8,64,32,64]{3,1,2,0:T(8,128)(2,1)} %get-tuple-element.831), channel_id=1, source_target_pairs={{0,1},{1,2},{2,3},{3,4},{4,5},{5,6},{6,7},{7,0},{8,9},{9,10},{10,1... | collective-permute-start | bytes 6291464 | tf_op jit(solution)/shard_map/while/body/eval_jaxpr/ppermute | solution.py:103
  2408.2 315.0 %collective-permute-start.3 = (f32[8,64,32,64]{3,1,2,0:T(8,128)}, f32[8,64,32,64]{3,1,2,0:T(8,128)}, u32[]{:S(2)}, u32[]{:S(2)}) collective-permute-start(f32[8,64,32,64]{3,1,2,0:T(8,128)} %get-tuple-element.834), channel_id=1, source_target_pairs={{0,1},{1,2},{2,3},{3,4},{4,5},{5,6},{6,7},{7,0},{8,9},{9,10},{10,1... | collective-permute-start | bytes 12582920 | tf_op jit(solution)/shard_map/while/body/eval_jaxpr/ppermute | solution.py:106
  2408.2 315.0 %collective-permute-start.2 = (f32[8,64,32,64]{3,1,2,0:T(8,128)}, f32[8,64,32,64]{3,1,2,0:T(8,128)}, u32[]{:S(2)}, u32[]{:S(2)}) collective-permute-start(f32[8,64,32,64]{3,1,2,0:T(8,128)} %get-tuple-element.833), channel_id=1, source_target_pairs={{0,1},{1,2},{2,3},{3,4},{4,5},{5,6},{6,7},{7,0},{8,9},{9,10},{10,1... | collective-permute-start | bytes 12582920 | tf_op jit(solution)/shard_map/while/body/eval_jaxpr/ppermute | solution.py:105
  2408.2 264.8 %collective-permute-start.5 = (bf16[8,64,32,64]{3,1,2,0:T(8,128)(2,1)}, bf16[8,64,32,64]{3,1,2,0:T(8,128)(2,1)}, u32[]{:S(2)}, u32[]{:S(2)}) collective-permute-start(bf16[8,64,32,64]{3,1,2,0:T(8,128)(2,1)} %get-tuple-element.832), channel_id=1, source_target_pairs={{0,1},{1,2},{2,3},{3,4},{4,5},{5,6},{6,7},{7,0},{8,9},{9,10},{10,1... | collective-permute-start | bytes 6291464 | tf_op jit(solution)/shard_map/while/body/eval_jaxpr/ppermute | solution.py:104
  2408.2 309.7 %collective-permute-start.4 = (bf16[8,64,32,64]{3,1,2,0:T(8,128)(2,1)}, bf16[8,64,32,64]{3,1,2,0:T(8,128)(2,1)}, u32[]{:S(2)}, u32[]{:S(2)}) collective-permute-start(bf16[8,64,32,64]{3,1,2,0:T(8,128)(2,1)} %get-tuple-element.831), channel_id=1, source_target_pairs={{0,1},{1,2},{2,3},{3,4},{4,5},{5,6},{6,7},{7,0},{8,9},{9,10},{10,1... | collective-permute-start | bytes 6291464 | tf_op jit(solution)/shard_map/while/body/eval_jaxpr/ppermute | solution.py:103
  2739.8 315.0 %collective-permute-start.3 = (f32[8,64,32,64]{3,1,2,0:T(8,128)}, f32[8,64,32,64]{3,1,2,0:T(8,128)}, u32[]{:S(2)}, u32[]{:S(2)}) collective-permute-start(f32[8,64,32,64]{3,1,2,0:T(8,128)} %get-tuple-element.834), channel_id=1, source_target_pairs={{0,1},{1,2},{2,3},{3,4},{4,5},{5,6},{6,7},{7,0},{8,9},{9,10},{10,1... | collective-permute-start | bytes 12582920 | tf_op jit(solution)/shard_map/while/body/eval_jaxpr/ppermute | solution.py:106
  2739.8 315.0 %collective-permute-start.2 = (f32[8,64,32,64]{3,1,2,0:T(8,128)}, f32[8,64,32,64]{3,1,2,0:T(8,128)}, u32[]{:S(2)}, u32[]{:S(2)}) collective-permute-start(f32[8,64,32,64]{3,1,2,0:T(8,128)} %get-tuple-element.833), channel_id=1, source_target_pairs={{0,1},{1,2},{2,3},{3,4},{4,5},{5,6},{6,7},{7,0},{8,9},{9,10},{10,1... | collective-permute-start | bytes 12582920 | tf_op jit(solution)/shard_map/while/body/eval_jaxpr/ppermute | solution.py:105
  2739.8 264.8 %collective-permute-start.5 = (bf16[8,64,32,64]{3,1,2,0:T(8,128)(2,1)}, bf16[8,64,32,64]{3,1,2,0:T(8,128)(2,1)}, u32[]{:S(2)}, u32[]{:S(2)}) collective-permute-start(bf16[8,64,32,64]{3,1,2,0:T(8,128)(2,1)} %get-tuple-element.832), channel_id=1, source_target_pairs={{0,1},{1,2},{2,3},{3,4},{4,5},{5,6},{6,7},{7,0},{8,9},{9,10},{10,1... | collective-permute-start | bytes 6291464 | tf_op jit(solution)/shard_map/while/body/eval_jaxpr/ppermute | solution.py:104
  2739.8 309.7 %collective-permute-start.4 = (bf16[8,64,32,64]{3,1,2,0:T(8,128)(2,1)}, bf16[8,64,32,64]{3,1,2,0:T(8,128)(2,1)}, u32[]{:S(2)}, u32[]{:S(2)}) collective-permute-start(bf16[8,64,32,64]{3,1,2,0:T(8,128)(2,1)} %get-tuple-element.831), channel_id=1, source_target_pairs={{0,1},{1,2},{2,3},{3,4},{4,5},{5,6},{6,7},{7,0},{8,9},{9,10},{10,1... | collective-permute-start | bytes 6291464 | tf_op jit(solution)/shard_map/while/body/eval_jaxpr/ppermute | solution.py:103
  3071.4 315.0 %collective-permute-start.3 = (f32[8,64,32,64]{3,1,2,0:T(8,128)}, f32[8,64,32,64]{3,1,2,0:T(8,128)}, u32[]{:S(2)}, u32[]{:S(2)}) collective-permute-start(f32[8,64,32,64]{3,1,2,0:T(8,128)} %get-tuple-element.834), channel_id=1, source_target_pairs={{0,1},{1,2},{2,3},{3,4},{4,5},{5,6},{6,7},{7,0},{8,9},{9,10},{10,1... | collective-permute-start | bytes 12582920 | tf_op jit(solution)/shard_map/while/body/eval_jaxpr/ppermute | solution.py:106
  3071.4 315.0 %collective-permute-start.2 = (f32[8,64,32,64]{3,1,2,0:T(8,128)}, f32[8,64,32,64]{3,1,2,0:T(8,128)}, u32[]{:S(2)}, u32[]{:S(2)}) collective-permute-start(f32[8,64,32,64]{3,1,2,0:T(8,128)} %get-tuple-element.833), channel_id=1, source_target_pairs={{0,1},{1,2},{2,3},{3,4},{4,5},{5,6},{6,7},{7,0},{8,9},{9,10},{10,1... | collective-permute-start | bytes 12582920 | tf_op jit(solution)/shard_map/while/body/eval_jaxpr/ppermute | solution.py:105
  3071.4 264.8 %collective-permute-start.5 = (bf16[8,64,32,64]{3,1,2,0:T(8,128)(2,1)}, bf16[8,64,32,64]{3,1,2,0:T(8,128)(2,1)}, u32[]{:S(2)}, u32[]{:S(2)}) collective-permute-start(bf16[8,64,32,64]{3,1,2,0:T(8,128)(2,1)} %get-tuple-element.832), channel_id=1, source_target_pairs={{0,1},{1,2},{2,3},{3,4},{4,5},{5,6},{6,7},{7,0},{8,9},{9,10},{10,1... | collective-permute-start | bytes 6291464 | tf_op jit(solution)/shard_map/while/body/eval_jaxpr/ppermute | solution.py:104
  3071.4 309.7 %collective-permute-start.4 = (bf16[8,64,32,64]{3,1,2,0:T(8,128)(2,1)}, bf16[8,64,32,64]{3,1,2,0:T(8,128)(2,1)}, u32[]{:S(2)}, u32[]{:S(2)}) collective-permute-start(bf16[8,64,32,64]{3,1,2,0:T(8,128)(2,1)} %get-tuple-element.831), channel_id=1, source_target_pairs={{0,1},{1,2},{2,3},{3,4},{4,5},{5,6},{6,7},{7,0},{8,9},{9,10},{10,1... | collective-permute-start | bytes 6291464 | tf_op jit(solution)/shard_map/while/body/eval_jaxpr/ppermute | solution.py:103
  3403.4 130.1 %collective-permute-start.6 = (f32[8,64,32,64]{3,1,2,0:T(8,128)}, f32[8,64,32,64]{3,1,2,0:T(8,128)}, u32[]{:S(2)}, u32[]{:S(2)}) collective-permute-start(f32[8,64,32,64]{3,1,2,0:T(8,128)} %get-tuple-element.507), channel_id=1, source_target_pairs={{0,1},{1,2},{2,3},{3,4},{4,5},{5,6},{6,7},{7,0},{8,9},{9,10},{10,1... | collective-permute-start | bytes 12582920 | tf_op jit(solution)/shard_map/ppermute | solution.py:118
  3410.2 168.3 %collective-permute-start.7 = (bf16[8,64,32,64]{3,1,2,0:T(8,128)(2,1)}, bf16[8,64,32,64]{3,1,2,0:T(8,128)(2,1)}, u32[]{:S(2)}, u32[]{:S(2)}) collective-permute-start(bf16[8,64,32,64]{3,1,2,0:T(8,128)(2,1)} %convert.17), channel_id=1, source_target_pairs={{0,1},{1,2},{2,3},{3,4},{4,5},{5,6},{6,7},{7,0},{8,9},{9,10},{10,1... | collective-permute-start | bytes 6291464 | tf_op jit(solution)/shard_map/ppermute | solution.py:119
  (39 other events, 1495.3 us)
Sparse Core Ops, SparseCore 0:
  3636.5 646.6 all-reduce.2
where the time goes:
time: 4350 us; the launch traced here: 4340 us
  waiting for transfers between devices  3500 us (80%)
  local copies, waits for them, and re-layouts  476 us (11%)
  matrix products  140 us (3%)
  other arithmetic  121 us (3%)
  starting transfers between devices  66.9 us (2%)
    ppermute x7, waiting for transfers between devices, bwd_step(): v_cur = lax.ppermute(v_cur, 'cp', shift_perm)  1820 us
    psum x1, waiting for transfers between devices, device_fn(): g_gain, g_wqkv, g_wout = lax.psum((g_gain, g_wqkv, g_wout), 'cp')  599 us
    ppermute x7, waiting for transfers between devices, fwd_step(): v_cur = lax.ppermute(v_cur, 'cp', shift_perm)  390 us
    ppermute x7, waiting for transfers between devices, fwd_step(): k_cur = lax.ppermute(k_cur, 'cp', shift_perm)  315 us
    ppermute x7, waiting for transfers between devices, bwd_step(): k_cur = lax.ppermute(k_cur, 'cp', shift_perm)  278 us
    while x42, local copies, waits for them, and re-layouts  263 us
    ppermute x1, waiting for transfers between devices, device_fn(): dk_home = lax.ppermute(dk_cur, 'cp', shift_perm)  102 us
  transfers between devices with their start and end apart: 45, of which 31 were waited for; matrix products, arithmetic and copies ran while one was open for 4% of the time, Pallas kernels for 0%

commit v1 on v0

v1 whole, which is shorter than its diff:
```python
import functools
import math

import jax
import jax.numpy as jnp
from jax import lax
from jax.experimental import pallas as pl
from jax.experimental.pallas import tpu as pltpu
from jax.sharding import PartitionSpec as P

NORM_EPS = 1e-5
MSCALE = math.sqrt(1.0 + math.log(32.0) / math.log(4096.0))
MASK_VALUE = -1e30
F32, BF = jnp.float32, jnp.bfloat16
HD = 64
HALF = HD // 2
GW = 256
GH = GW // HD
NT = (((1,), (1,)), ((), ()))


def dot(a, b):
    return jnp.dot(a, b, preferred_element_type=F32)


def dot_nt(a, b):
    return lax.dot_general(a, b, NT, preferred_element_type=F32)


def rope_t(t, c, s):
    out = []
    for h in range(0, t.shape[0], HD):
        a, b = t[h:h + HALF], t[h + HALF:h + HD]
        out += [a * c - b * s, b * c + a * s]
    return jnp.concatenate(out, axis=0)


class Refs:
    pass


def projection(S, r_ref, gy_ref, ws, c, s):
    wq, wk, wv, wo = ws

    def q():
        S.qT[...] = rope_t(dot(r_ref[...], wq[...]).T, c[...], s[...]).astype(BF)

    def k():
        t = rope_t(dot(r_ref[...], wk[...]).T, c[...], s[...]).astype(BF)
        S.kT[...] = t
        S.kb[...] = t.T

    def v():
        t = dot(r_ref[...], wv[...]).astype(BF)
        S.vb[...] = t
        S.vT[...] = t.T

    def d():
        S.doT[...] = dot_nt(gy_ref[...], wo[...]).astype(BF).T

    return [q, k, v, d]


def attention(S, X, outs, c, s):
    o_out, oT_out, dq_out, dk_out, dv_out = outs
    T = S.kb.shape[0]
    HB = T // 2
    scale = 1.0 / math.sqrt(HD)
    kappa = scale * math.log2(math.e)
    keep = lax.broadcasted_iota(jnp.int32, (HB, HB), 0) <= lax.broadcasted_iota(jnp.int32, (HB, HB), 1)
    mxs = {}
    CH = 32

    def padrows(t, h):
        parts = []
        if h:
            parts.append(jnp.zeros((HD * h, t.shape[1]), BF))
        parts.append(t)
        if h < GH - 1:
            parts.append(jnp.zeros((HD * (GH - 1 - h), t.shape[1]), BF))
        return jnp.concatenate(parts, axis=0)

    def tiles():
        for qt in range(2):
            yield qt, HB * (qt + 1), slice(qt * HB, (qt + 1) * HB)

    def scores(h):
        SS, DP, hs = X.ss[h & 1], X.dd[h & 1], slice(HD * h, HD * h + HD)
        for qt, L, qs in tiles():
            st = dot(S.kb[:L, :], padrows(S.qT[hs, qs], h))
            diag = jnp.where(keep, st[L - HB:], MASK_VALUE)
            SS[L - HB:L, qs] = diag
            mx = jnp.max(diag, axis=0, keepdims=True)
            if qt:
                SS[:L - HB, qs] = st[:L - HB]
                mx = jnp.maximum(mx, jnp.max(st[:L - HB], axis=0, keepdims=True))
            mxs[h, qt] = mx * kappa
            DP[:L, qs] = dot(S.vb[:L, :], padrows(S.doT[hs, qs], h))

    def softmax(h):
        SS, PB = X.ss[h & 1], X.pp[h & 1]
        for qt, L, qs in tiles():
            acc = jnp.zeros((8, HB), F32)
            for i in range(0, L, CH):
                e = jnp.exp2(SS[i:i + CH, qs] * kappa - mxs[h, qt])
                acc = acc + jnp.sum(e.reshape(CH // 8, 8, HB), axis=0)
                SS[i:i + CH, qs] = e
            inv = 1.0 / jnp.sum(acc, axis=0, keepdims=True)
            for i in range(0, L, CH):
                p = SS[i:i + CH, qs] * inv
                SS[i:i + CH, qs] = p
                PB[i:i + CH, qs] = p.astype(BF)

    def d_scores(h):
        SS, DP, PB, DS = X.ss[h & 1], X.dd[h & 1], X.pp[h & 1], X.ds[h & 1]
        hs = slice(HD * h, HD * h + HD)
        for qt, L, qs in tiles():
            oh = dot(S.vT[hs, :L], PB[:L, qs])
            X.oT[hs, qs] = oh
            delta = jnp.sum(oh * S.doT[hs, qs].astype(F32), axis=0, keepdims=True)
            for i in range(0, L, CH):
                DS[i:i + CH, qs] = (SS[i:i + CH, qs] * (DP[i:i + CH, qs] - delta)).astype(BF)

    def grads(h):
        PB, DS = X.pp[h & 1], X.ds[h & 1]
        hs = slice(HD * h, HD * h + HD)
        X.dvT[hs, :HB] = dot_nt(S.doT[hs, :], PB[:HB, :])
        X.dvT[hs, HB:] = dot_nt(S.doT[hs, HB:], PB[HB:, HB:])
        for qt, L, qs in tiles():
            X.dqT[hs, qs] = dot(S.kT[hs, :L], DS[:L, qs])
        X.dkT[hs, :HB] = dot_nt(S.qT[hs, :], DS[:HB, :])
        X.dkT[hs, HB:] = dot_nt(S.qT[hs, HB:], DS[HB:, HB:])

    def finish():
        ot = X.oT[...].astype(BF)
        oT_out[...] = ot
        o_out[...] = ot.T
        cc, sc = c[...] * scale, s[...] * -scale
        dq_out[...] = rope_t(X.dqT[...], cc, sc).astype(BF).T
        dk_out[...] = rope_t(X.dkT[...], cc, sc).astype(BF).T
        dv_out[...] = X.dvT[...].astype(BF).T

    fp = functools.partial
    steps = [fp(scores, 0)]
    for h in range(GH):
        if h + 1 < GH:
            steps.append(fp(scores, h + 1))
        steps.append(fp(softmax, h))
        if h:
            steps.append(fp(grads, h - 1))
        steps.append(fp(d_scores, h))
    return steps + [fp(grads, GH - 1), finish]


def interleave(a, b):
    out, j = [], 0
    for i, f in enumerate(a):
        while j < len(b) and j * len(a) <= i * len(b):
            out.append(b[j])
            j += 1
        out.append(f)
    return out + b[j:]


def block_kernel(n_cp, n_seq, n_units, x_loc, gy_loc, tab_loc, gain, w_qkv, w_out,
                 x_all, gy_all, rT, o, oT, dq, dk, dv,
                 tab_all, cT, sT, wq, wk, wv, wo, xbuf, gybuf, rbuf, *rest):
    rest = list(rest)
    sets = []
    for _ in range(2):
        S = Refs()
        S.kb, S.vb, S.qT, S.kT, S.vT, S.doT = rest[:6]
        rest = rest[6:]
        sets.append(S)
    X = Refs()
    X.oT, X.dqT, X.dkT, X.dvT = rest[:4]
    X.ss, X.dd, X.pp, X.ds = rest[4:6], rest[6:8], rest[8:10], rest[10:12]
    send_sem, recv_sem, tab_send, tab_recv, w_sem, load_sem, put_sem = rest[12:]
    step = pl.program_id(0)
    n_steps = n_seq * n_units // 2
    spq = n_units // 2
    piece = x_loc.shape[1]
    T = n_cp * piece
    me = lax.axis_index('cp')
    chip, core = me // 2, me % 2
    n_chip = n_cp // 2
    right = lax.rem(chip + 1, n_chip) * 2 + core
    left = lax.rem(chip + n_chip - 1, n_chip) * 2 + core
    far = lax.rem(chip + 2, n_chip) * 2 + core
    mate = chip * 2 + (1 - core)
    XL, XR, XF, GL, GR, GF, XP, GP = range(8)

    def rows(q, dev):
        return pl.ds(pl.multiple_of(q * T + dev * piece, piece), piece)

    def send(src, dst, q, slot, to):
        pltpu.make_async_remote_copy(src_ref=src, dst_ref=dst, send_sem=send_sem.at[q], recv_sem=recv_sem.at[q, slot],
                                     device_id={'cp': to}, device_id_type=pl.DeviceIdType.MESH).start()

    def arrived(arr, q, slot, n=1):
        ref = arr.at[pl.ds(0, n * piece)]
        pltpu.make_async_copy(ref, ref, recv_sem.at[q, slot]).wait()

    def send_own(q):
        for loc, arr, from_left, from_right, from_mate in ((x_loc, x_all, XL, XR, XP), (gy_loc, gy_all, GL, GR, GP)):
            dst = arr.at[rows(q, me)]
            send(loc.at[q], dst, q, from_left, right)
            send(loc.at[q], dst, q, from_right, left)
            send(loc.at[q], dst, q, from_mate, mate)

    def relay_near(q):
        arrived(x_all, q, XL)
        src = x_all.at[rows(q, left)]
        send(src, src, q, XF, right)
        send(src, src, q, XP, mate)
        arrived(x_all, q, XR)
        src = x_all.at[rows(q, right)]
        send(src, src, q, XP, mate)
        arrived(gy_all, q, GR)
        src = gy_all.at[rows(q, right)]
        send(src, src, q, GF, left)
        send(src, src, q, GP, mate)
        arrived(gy_all, q, GL)
        src = gy_all.at[rows(q, left)]
        send(src, src, q, GP, mate)

    def relay_far(q):
        arrived(x_all, q, XF)
        src = x_all.at[rows(q, far)]
        send(src, src, q, XP, mate)
        arrived(gy_all, q, GF)
        src = gy_all.at[rows(q, far)]
        send(src, src, q, GP, mate)

    def load(q):
        arrived(x_all, q, XP, n_chip)
        arrived(gy_all, q, GP, n_chip)
        slot = lax.rem(q, 2)
        for p in range(n_cp):
            at = pl.ds(p * piece, piece)

            @pl.when(p == me)
            def _():
                pltpu.make_async_copy(x_loc.at[q], xbuf.at[at], load_sem.at[0]).start()
                pltpu.make_async_copy(gy_loc.at[q], gybuf.at[slot, at], load_sem.at[1]).start()

            @pl.when(p != me)
            def _():
                pltpu.make_async_copy(x_all.at[rows(q, p)], xbuf.at[at], load_sem.at[0]).start()
                pltpu.make_async_copy(gy_all.at[rows(q, p)], gybuf.at[slot, at], load_sem.at[1]).start()

    def put_own(q):
        at = pl.ds(pl.multiple_of(me * piece, piece), piece)
        return pltpu.make_async_copy(gybuf.at[lax.rem(q, 2), at], gy_all.at[rows(q, me)], put_sem)

    def normalize(q):
        pltpu.make_async_copy(xbuf, xbuf, load_sem.at[0]).wait()
        pltpu.make_async_copy(gybuf.at[0], gybuf.at[0], load_sem.at[1]).wait()
        put_own(q).start()
        slot = lax.rem(q, 2)

        def chunk(i, _):
            i = pl.multiple_of(i * 128, 128)
            for j in range(0, 128, 16):
                xf = xbuf[pl.ds(i + j, 16), :].astype(F32)
                inv = lax.rsqrt(jnp.mean(xf * xf, axis=1, keepdims=True) + NORM_EPS)
                rbuf[slot, pl.ds(i + j, 16), :] = (xf * inv * gain[...]).astype(BF)
            rT[:, pl.ds(i, 128)] = rbuf[slot, pl.ds(i, 128), :].T
            return 0

        lax.fori_loop(0, T // 128, chunk, 0)

    @pl.when(step == 0)
    def _():
        width = n_units * GW
        at = pl.multiple_of(core * width, width)
        loads = [pltpu.make_async_copy(w_qkv.at[:, pl.ds(pl.multiple_of(i * 2 * width + at, width), width)], buf, w_sem.at[i])
                 for i, buf in enumerate((wq, wk, wv))]
        loads.append(pltpu.make_async_copy(w_out.at[pl.ds(at, width), :], wo, w_sem.at[3]))
        for cp in loads:
            cp.start()
        barrier = pltpu.get_barrier_semaphore()
        for d in range(1, n_cp):
            pl.semaphore_signal(barrier, inc=1, device_id={'cp': lax.rem(me + d, n_cp)}, device_id_type=pl.DeviceIdType.MESH)
        pl.semaphore_wait(barrier, n_cp - 1)
        mine = pl.ds(pl.multiple_of(me * piece, piece), piece)
        for d in range(1, n_cp):
            pltpu.make_async_remote_copy(src_ref=tab_loc, dst_ref=tab_all.at[mine], send_sem=tab_send, recv_sem=tab_recv,
                                         device_id={'cp': lax.rem(me + d, n_cp)}, device_id_type=pl.DeviceIdType.MESH).start()
        send_own(0)
        tab_all[mine, :] = tab_loc[...]
        relay_near(0)
        send_own(1)
        relay_far(0)
        load(0)
        others = tab_all.at[pl.ds(0, (n_cp - 1) * piece)]
        pltpu.make_async_copy(others, others, tab_recv).wait()
        pltpu.make_async_copy(others, others, tab_send).wait()
        tab = tab_all[...].T
        cT[...] = tab[:HALF]
        sT[...] = tab[HALF:2 * HALF]
        normalize(0)
        for cp in loads:
            cp.wait()
        for f in projection(sets[0], rbuf.at[0], gybuf.at[0], [t.at[:, pl.ds(0, GW)] for t in (wq, wk, wv)] + [wo.at[pl.ds(0, GW), :]], cT, sT):
            f()

    seq = step // spq
    first = lax.rem(step, spq) == 0
    nxt = seq + 1

    @pl.when(first & (nxt < n_seq))
    def _():
        relay_near(nxt)

    @pl.when(first & (nxt + 1 < n_seq))
    def _():
        send_own(nxt + 1)

    def weights(u):
        at = pl.ds(pl.multiple_of(u * GW, GW), GW)
        return [t.at[:, at] for t in (wq, wk, wv)] + [wo.at[at, :]]

    def half_step(u, unit_next):
        cs = pl.ds(u * GW, GW)
        outs = [o.at[0, :, cs], oT.at[cs, :]] + [t.at[0, :, cs] for t in (dq, dk, dv)]
        un = lax.rem(unit_next, n_units)
        slot = lax.rem(unit_next // n_units, 2)
        for f in interleave(attention(sets[u], X, outs, cT, sT),
                            projection(sets[1 - u], rbuf.at[slot], gybuf.at[slot], weights(un), cT, sT)):
            f()

    half_step(0, step * 2 + 1)

    @pl.when(first & (nxt < n_seq))
    def _():
        relay_far(nxt)

    @pl.when(jnp.logical_not(first) & (nxt < n_seq))
    def _():
        put_own(seq).wait()
        load(nxt)
        normalize(nxt)

    half_step(1, step * 2 + 2)

    @pl.when(step == n_steps - 1)
    def _():
        put_own(n_seq - 1).wait()
        for q in range(n_seq):
            ref = x_all.at[pl.ds(0, (6 + 3 * n_chip - 4) * piece)]
            pltpu.make_async_copy(ref, ref, send_sem.at[q]).wait()


def block_call(x, gy, tab, gain, w_qkv, w_out, n_cp):
    n_seq, piece, D = x.shape
    T = n_cp * piece
    W = w_out.shape[0] // 2
    n_units = W // GW
    spq = n_units // 2
    n_steps = n_seq * spq
    V = pltpu.VMEM
    any_spec = pl.BlockSpec(memory_space=pl.ANY)
    whole = pl.BlockSpec(memory_space=pltpu.VMEM)
    act = pl.BlockSpec((1, T, 2 * GW), lambda j: (j // spq, 0, lax.rem(j, spq)))
    N = n_seq * T
    return pl.pallas_call(
        functools.partial(block_kernel, n_cp, n_seq, n_units),
        grid=(n_steps,),
        in_specs=[any_spec, any_spec, whole, whole, any_spec, any_spec],
        out_specs=[any_spec, any_spec, pl.BlockSpec((D, T), lambda j: (0, jnp.minimum((j + spq - 1) // spq, n_seq - 1))),
                   act, pl.BlockSpec((2 * GW, T), lambda j: (lax.rem(j, spq), j // spq)), act, act, act],
        out_shape=[jax.ShapeDtypeStruct((N, D), BF), jax.ShapeDtypeStruct((N, D), BF), jax.ShapeDtypeStruct((D, N), BF),
                   jax.ShapeDtypeStruct((n_seq, T, W), BF), jax.ShapeDtypeStruct((W, N), BF)]
        + [jax.ShapeDtypeStruct((n_seq, T, W), BF)] * 3,
        scratch_shapes=[V((T, 128), F32), V((HALF, T), F32), V((HALF, T), F32), V((D, W), BF), V((D, W), BF), V((D, W), BF), V((W, D), BF),
                        V((T, D), BF), V((2, T, D), BF), V((2, T, D), BF)]
        + ([V((T, GW), BF)] * 2 + [V((GW, T), BF)] * 4) * 2 + [V((GW, T), F32)] * 4 + [V((T, T), F32)] * 4 + [V((T, T), BF)] * 4
        + [pltpu.SemaphoreType.DMA((n_seq,)), pltpu.SemaphoreType.DMA((n_seq, 8)), pltpu.SemaphoreType.DMA, pltpu.SemaphoreType.DMA,
           pltpu.SemaphoreType.DMA((4,)), pltpu.SemaphoreType.DMA((2,)), pltpu.SemaphoreType.DMA],
        compiler_params=pltpu.CompilerParams(vmem_limit_bytes=63 * 1024 * 1024, collective_id=0, has_side_effects=True,
                                             dimension_semantics=("arbitrary",)),
        name="block",
    )(x, gy, tab, gain, w_qkv, w_out)


def wgrad_kernel(spec, *refs):
    M, N, K, BM, BK, n_g, n_in, copies, own, rhs_col = spec
    refs = list(refs)
    lhs, rhs = refs[:2] if M else (None, None)
    recvs = refs[2 if M else 0:][:len(copies)]
    outs = refs[n_in:]
    send, gs = (outs[0], outs[1:1 + n_g]) if M else (None, outs[:n_g])
    scr = outs[(1 if M else 0) + n_g:]
    core = lax.rem(lax.axis_index('cp'), 2)
    step = pl.program_id(0)
    PR, NSLOT = 128, 4
    if copies:
        bounce, in_sem, out_sem = scr[-3:]
        scr = scr[:-3]

    pieces = [(i, r) for i, c in enumerate(copies) for r in range(0, c[1], PR)]
    nk = K // BK if M else 1
    n_steps = (M // BM) * nk if M else 1

    def piece(p, out):
        i, r = pieces[p]
        g, rows, cols, row0, col0 = copies[i]
        buf = bounce.at[p % NSLOT, :, pl.ds(0, cols)]
        at_r, at_c = row0(1 - core), col0(1 - core)
        dst = gs[g].at[pl.ds(pl.multiple_of(at_r + r, PR), PR), pl.ds(pl.multiple_of(at_c, 128), cols)]
        if out:
            return pltpu.make_async_copy(buf, dst, out_sem.at[p % NSLOT])
        return pltpu.make_async_copy(recvs[i].at[pl.ds(r, PR), :], buf, in_sem.at[p % NSLOT])

    def copy_slot(p):
        if p < len(pieces):
            if p >= NSLOT:
                piece(p - NSLOT, True).wait()
            piece(p, False).start()
        if 0 <= p - 2 < len(pieces):
            piece(p - 2, False).wait()
            piece(p - 2, True).start()

    if not M:
        for p in range(len(pieces) + 2):
            copy_slot(p)
        for p in range(max(0, len(pieces) - NSLOT), len(pieces)):
            piece(p, True).wait()
        return

    wbuf, acc, w_sem, o_sem = scr
    m, k = step // nk, lax.rem(step, nk)
    slot = lax.rem(m, 2)

    def w_load(i):
        at = pl.ds(i * BK, BK)
        return pltpu.make_async_copy(rhs.at[at, pl.ds(rhs_col, N)], wbuf.at[at], w_sem.at[i])

    def put(mm, sl):
        g, row0, col0 = own
        src = acc.at[sl]
        at = pl.ds(pl.multiple_of(mm * BM, BM), BM)
        dst = gs[g].at[pl.ds(pl.multiple_of(row0(core) + mm * BM, BM), BM), pl.ds(pl.multiple_of(col0(core), 128), N)]
        return pltpu.make_async_copy(src, send.at[at], o_sem.at[sl, 0]), pltpu.make_async_copy(src, dst, o_sem.at[sl, 1])

    @pl.when(step == 0)
    def _():
        for i in range(nk):
            w_load(i).start()

    for s in range(n_steps):
        lo, hi = (len(pieces) + 2) * s // n_steps, (len(pieces) + 2) * (s + 1) // n_steps
        if hi > lo and copies:
            @pl.when(step == s)
            def _():
                for p in range(lo, hi):
                    copy_slot(p)

    for i in range(nk):
        @pl.when(step == i)
        def _():
            w_load(i).wait()

    @pl.when((k == 0) & (m >= 2))
    def _():
        for cp in put(m - 2, slot):
            cp.wait()

    w = wbuf.at[pl.ds(pl.multiple_of(k * BK, BK), BK)]

    @pl.when(k == 0)
    def _():
        acc[slot] = dot(lhs[...], w[...])

    @pl.when(k > 0)
    def _():
        acc[slot] += dot(lhs[...], w[...])

    @pl.when(k == nk - 1)
    def _():
        for cp in put(m, slot):
            cp.start()

    @pl.when(step == n_steps - 1)
    def _():
        for mm in range(max(0, M // BM - 2), M // BM):
            for cp in put(mm, mm % 2):
                cp.wait()
        for p in range(max(0, len(pieces) - NSLOT), len(pieces)):
            piece(p, True).wait()


def wgrad_call(name, lhs, rhs, n, rhs_col, own, gs, shapes, copies, BM=512, BK=1024):
    V = pltpu.VMEM
    any_spec = pl.BlockSpec(memory_space=pl.ANY)
    args, in_specs, out_specs, out_shape, scratch = [], [], [], [], []
    M = K = 0
    if lhs is not None:
        M, K = lhs.shape
        nk = K // BK
        args += [lhs, rhs]
        in_specs += [pl.BlockSpec((BM, BK), lambda j: (j // nk, lax.rem(j, nk))), any_spec]
        out_specs.append(any_spec)
        out_shape.append(jax.ShapeDtypeStruct((M, n), F32))
        scratch += [V((K, n), BF), V((2, BM, n), F32), pltpu.SemaphoreType.DMA((nk,)), pltpu.SemaphoreType.DMA((2, 2))]
    args += [c[0] for c in copies]
    in_specs += [any_spec] * len(copies)
    aliases = {}
    for i, g in enumerate(gs):
        if g is not None:
            aliases[len(args)] = len(out_shape)
            args.append(g)
            in_specs.append(any_spec)
        out_specs.append(any_spec)
        out_shape.append(jax.ShapeDtypeStruct(shapes[i], F32))
    if copies:
        wide = max(c[0].shape[1] for c in copies)
        scratch += [V((4, 128, wide), F32), pltpu.SemaphoreType.DMA((4,)), pltpu.SemaphoreType.DMA((4,))]
    spec = (M, n, K, BM, BK, len(gs), len(args), [(c[1], c[0].shape[0], c[0].shape[1], c[2], c[3]) for c in copies], own, rhs_col)
    return pl.pallas_call(
        functools.partial(wgrad_kernel, spec),
        grid=((M // BM) * (K // BK) if M else 1,),
        in_specs=in_specs, out_specs=out_specs, out_shape=out_shape, scratch_shapes=scratch,
        input_output_aliases=aliases,
        compiler_params=pltpu.CompilerParams(vmem_limit_bytes=40 * 1024 * 1024),
        cost_estimate=pl.CostEstimate(flops=2 * M * n * K, bytes_accessed=8 * M * n + 2 * (M * K + K * n), transcendentals=0),
        name=name,
    )(*args)


def solution(mesh):
    cp_size = mesh.shape['cp']
    swap = [(i, i ^ 1) for i in range(cp_size)]

    def device_fn(x_in, positions, long_factor, norm_gain, w_qkv, w_out, grad_y):
        batch, piece, hidden = x_in.shape
        width = w_out.shape[0]
        hw = width // 2
        me = lax.axis_index('cp')
        core = lax.rem(me, 2)
        half = long_factor.shape[0]
        exponent = jnp.arange(half, dtype=F32) * (1.0 / half)
        inv_freq = 1.0 / (long_factor * jnp.power(10000.0, exponent))
        angles = positions.astype(F32)[:, None] * inv_freq[None, :]
        tab = jnp.concatenate([jnp.cos(angles) * MSCALE, jnp.sin(angles) * MSCALE, jnp.zeros((piece, 128 - 2 * half), F32)], axis=1)
        _, gy_all, rT, o, oT, dq, dk, dv = block_call(x_in, grad_y, tab, norm_gain[None], w_qkv, w_out, cp_size)
        acts = (o, dq, dk, dv)
        mine = [lax.dynamic_slice_in_dim(t, me*piece, piece, 1) for t in acts]
        theirs = [lax.dynamic_slice_in_dim(t, (me ^ 1)*piece, piece, 1) for t in acts]
        got = [lax.ppermute(t, 'cp', swap) for t in theirs]

        def exchange(t):
            return lax.ppermute(t, 'cp', swap)

        zero = lambda c: 0
        at = lambda base: (lambda c: base + c * hw)
        flat = lambda t: t.reshape(-1, t.shape[2])
        s_qkv, s_out = (hidden, 3 * width), (width, hidden)
        send_o, g_out = wgrad_call('gw_out', oT, gy_all, hidden, 0, (0, at(0), zero), [None], [s_out], [])
        recv_o = exchange(send_o)
        send_v, g_qkv = wgrad_call('gw_v', rT, flat(dv), hw, 0, (0, zero, at(2 * width)), [None], [s_qkv], [])
        recv_v = exchange(send_v)
        send_k, g_qkv, g_out = wgrad_call('gw_k', rT, flat(dk), hw, 0, (0, zero, at(width)), [g_qkv, g_out], [s_qkv, s_out],
                                          [(recv_o, 1, at(0), zero)])
        recv_k = exchange(send_k)

        def join(a, b, axis):
            return jnp.concatenate([jnp.where(core == 0, a, b), jnp.where(core == 0, b, a)], axis=axis)

        o_own = join(mine[0], got[0], 2)
        d_qkv = jnp.concatenate([join(mine[i], got[i], 2) for i in (1, 2, 3)], axis=2)
        x_float = x_in.astype(F32)
        y_out = (x_float + jnp.einsum('bsh,hd->bsd', o_own, w_out, preferred_element_type=F32)).astype(BF)
        inv_rms = lax.rsqrt(jnp.mean(x_float * x_float, axis=-1, keepdims=True) + NORM_EPS)
        x_hat = x_float * inv_rms
        d_normed = jnp.einsum('bse,de->bsd', d_qkv, w_qkv, preferred_element_type=F32)
        g_gain = jnp.sum(d_normed * x_hat, axis=(0, 1))
        d = 1
        while d < cp_size:
            g_gain = g_gain + lax.ppermute(g_gain, 'cp', [(i, i ^ d) for i in range(cp_size)])
            d *= 2
        d_hat = d_normed * norm_gain
        dx_norm = inv_rms * (d_hat - x_hat * jnp.mean(d_hat * x_hat, axis=-1, keepdims=True))
        grad_x = (grad_y.astype(F32) + dx_norm).astype(BF)

        hq = hw // 2
        send_a, g_qkv = wgrad_call('gw_qa', rT, flat(dq), hq, 0, (0, zero, at(0)), [g_qkv], [s_qkv],
                                   [(recv_v, 0, zero, at(2 * width)), (recv_k, 0, zero, at(width))])
        recv_a = exchange(send_a)
        send_b, g_qkv = wgrad_call('gw_qb', rT, flat(dq), hq, hq, (0, zero, at(hq)), [g_qkv], [s_qkv], [])
        recv_b = exchange(send_b)
        (g_wqkv,) = wgrad_call('gw_end', None, None, 0, 0, None, [g_qkv], [s_qkv], [(recv_a, 0, zero, at(0)), (recv_b, 0, zero, at(hq))])
        return y_out, grad_x, g_gain, g_wqkv, g_out

    seq_spec = P('dp', 'cp', None)
    return jax.shard_map(device_fn, mesh=mesh, in_specs=(seq_spec, P(('dp', 'cp')), P(None), P(None), P(None, None), P(None, None), seq_spec), out_specs=(seq_spec, seq_spec, P('dp'), P('dp', None), P('dp', None)), check_vma=False)
```

time: 4350 us -> 479 us (0.11)
  waiting for transfers between devices: 3500 us -> 7.9 us
  local copies, waits for them, and re-layouts: 476 us -> 12 us
  Pallas kernels: 0 us -> 407 us
  matrix products: 140 us -> 26 us
  other arithmetic: 121 us -> 18.7 us
  starting transfers between devices: 66.9 us -> 4.86 us
    ppermute x44 -> x12, waiting for transfers between devices: 2900 us -> 7.9 us  [the longest x3 3.98 us: device_fn(): lax.ppermute(g_gain, 'cp', [(i, i ^ d) for i in range(cp_size)])]
    psum x1 -> x0, waiting for transfers between devices: 599 us -> none  [device_fn(): g_gain, g_wqkv, g_wout = lax.psum((g_gain, g_wqkv, g_wout), 'cp')]
    pallas_call x0 -> x7, Pallas kernels: none -> 407 us  [the longest x1 261 us: block_call(): pl.pallas_call(functools.partial(block_kernel, n_cp, n_seq, n_units), gri...]
    while x47 -> x0, local copies, waits for them, and re-layouts: 306 us -> none
    dot_general x12 -> x2, matrix products: 140 us -> 26 us  [the longest x1 20.2 us: device_fn(): jnp.einsum('bse,de->bsd', d_qkv, w_qkv, preferred_element_type=F32)]
    unnamed x57 -> x18, local copies, waits for them, and re-layouts: 64.7 us -> 2.71 us
    ppermute x44 -> x12, starting transfers between devices: 66.8 us -> 4.86 us  [the longest x3 2.25 us: device_fn(): lax.ppermute(g_gain, 'cp', [(i, i ^ d) for i in range(cp_size)])]
    reshape x5 -> x0, local copies, waits for them, and re-layouts: 56.1 us -> none  [the longest x1 20.4 us: device_fn(): qkv_proj = qkv_proj.reshape(batch, piece, 3, heads, head_dim)]
  transfers between devices with their start and end apart: 45 -> 12, of which waited for: 31 -> 3; matrix products, arithmetic and copies ran while one was open for 4% -> 11% of each run, Pallas kernels for 0% -> 22%
where the time goes in v1:
time: 479 us; the launch traced here: 477 us
  Pallas kernels  407 us (85%)
  matrix products  26 us (5%)
  other arithmetic  18.7 us (4%)
  local copies, waits for them, and re-layouts  12 us (3%)
  waiting for transfers between devices  7.9 us (2%)
  starting transfers between devices  4.86 us (1%)
    pallas_call x1, Pallas kernels, block_call(): pl.pallas_call(functools.partial(block_kernel, n_cp, n_seq, n_units), gri...  261 us
    pallas_call x6, Pallas kernels, wgrad_call(): pl.pallas_call(functools.partial(wgrad_kernel, spec), grid=(M // BM * (K...  145 us
    dot_general x1, matrix products, device_fn(): jnp.einsum('bse,de->bsd', d_qkv, w_qkv, preferred_element_type=F32)  20.2 us
  transfers between devices with their start and end apart: 12, of which 3 were waited for; matrix products, arithmetic and copies ran while one was open for 11% of the time, Pallas kernels for 22%

profile of v1, /device:TPU:112, one launch (start us, length us, event | category | flops | bytes accessed | tf_op | source)
XLA Modules:
  0.0 477.1 jit_solution(553709299965412286)
XLA Ops:
  0.6 0.7 convert_element_type.16
  1.3 0.7 multiply_divide_fusion
  2.2 0.7 maximum_maximum_fusion.tab_loc
  2.9 261.1 %block.1 = (bf16[4096,2048]{1,0:T(8,128)(2,1)}, bf16[4096,2048]{1,0:T(8,128)(2,1)}, bf16[2048,4096]{1,0:T(8,128)(2,1)}, bf16[8,512,1024]{2,1,0:T(8,128)(2,1)}, b...) custom-call(bf16[8,64,2048]{2,1,0:T(8,128)(2,1)} %x_loc.1, ...), custom_call_target="tpu_custom_call" | custom-call | tf_op jit(solution)/shard_map/block/pallas_call | solution.py:367
  264.0 25.3 %gw_out.1 = (f32[1024,2048]{1,0:T(8,128)S(1)}, f32[2048,2048]{1,0:T(8,128)}) custom-call(bf16[1024,4096]{1,0:T(8,128)(2,1)} %get-tuple-element.29.refs_0_, bf16[4096,2048]{1,0:T(8,128)(2,1)} %get-tuple-element.30.refs_1_), custom_call_target="tpu_custom_call" | custom-call | flops 17179869184 | bytes 41943040 | tf_op jit(solution)/shard_map/gw_out/pallas_call | solution.py:521
  289.4 28.0 %gw_v.1 = (f32[2048,1024]{1,0:T(8,128)}, f32[2048,6144]{1,0:T(8,128)}) custom-call(bf16[2048,4096]{1,0:T(8,128)(2,1)} %get-tuple-element.27.refs_0_, bf16[4096,1024]{1,0:T(8,128)(2,1)} %bitcast.22), custom_call_target="tpu_custom_call" | custom-call | flops 17179869184 | bytes 41943040 | tf_op jit(solution)/shard_map/gw_v/pallas_call | solution.py:521
  317.4 0.5 collective-permute-start.7
  317.9 29.4 %gw_k.1 = (f32[2048,1024]{1,0:T(8,128)}, f32[2048,6144]{1,0:T(8,128)}, f32[2048,2048]{1,0:T(8,128)}) custom-call(bf16[2048,4096]{1,0:T(8,128)(2,1)} %get-tuple-element.27.refs_0_, bf16[4096,1024]{1,0:T(8,128)(2,1)} %bitcast.19, f32[1024,2048]{1,0:T(8,128)} %collective-permute-done.8.refs_2_, ...), custom_call_target="tpu_custom_call", output_to_operand_aliasing={{1}: (3, {}), {2}: (4, {})} | custom-call | flops 17179869184 | bytes 41943040 | tf_op jit(solution)/shard_map/gw_k/pallas_call | solution.py:521
  347.5 2.4 constant_dynamic-slice_fusion.2
  350.3 2.3 constant_dynamic-slice_fusion
  352.7 2.3 constant_dynamic-slice_fusion.1
  355.4 2.3 constant_dynamic-slice_fusion.3
  358.1 3.9 collective-permute-done.1
  362.2 1.7 select_dynamic-update-slice_fusion.5
  363.9 2.1 select_dynamic-update-slice_fusion.4
  366.0 1.7 select_dynamic-update-slice_fusion.3
  367.7 2.1 select_dynamic-update-slice_fusion.2
  369.9 1.6 select_dynamic-update-slice_fusion.1
  371.5 1.6 select_dynamic-update-slice_fusion
  373.1 2.7 copy-done.3
  375.8 28.6 %gw_qa.1 = (f32[2048,512]{1,0:T(8,128)}, f32[2048,6144]{1,0:T(8,128)}) custom-call(bf16[2048,4096]{1,0:T(8,128)(2,1)} %get-tuple-element.27.refs_0_, bf16[4096,1024]{1,0:T(8,128)(2,1)S(1)} %bitcast.17, f32[2048,1024]{1,0:T(8,128)} %collective-permute-done.7.refs_2_, f32[2048,1024]{1,0:T(8,128)} %collective-permute-done.9.refs_3_, ...), custom_call_target="tpu_custom_call", output_to_operand_aliasing={{1}: (4, {})} | custom-call | flops 8589934592 | bytes 29360128 | tf_op jit(solution)/shard_map/gw_qa/pallas_call | solution.py:521
  404.9 20.8 %gw_qb.1 = (f32[2048,512]{1,0:T(8,128)}, f32[2048,6144]{1,0:T(8,128)}) custom-call(bf16[2048,4096]{1,0:T(8,128)(2,1)} %get-tuple-element.27.refs_0_, bf16[4096,1024]{1,0:T(8,128)(2,1)S(1)} %bitcast.18, f32[2048,6144]{1,0:T(8,128)} %get-tuple-element.37.refs_2_), custom_call_target="tpu_custom_call", output_to_operand_aliasing={{1}: (2, {})} | custom-call | flops 8589934592 | bytes 29360128 | tf_op jit(solution)/shard_map/gw_qb/pallas_call | solution.py:521
  426.1 20.2 %fusion.12 = (f32[2048]{0:T(1024)S(1)}, f32[8,64]{1,0:T(8,128)S(1)}, f32[8,64,2048]{2,1,0:T(8,128)}) fusion(bf16[8,64,2048]{2,1,0:T(8,128)(2,1)S(1)} %copy-done, f32[8,64]{1,0:T(8,128)S(1)} %add_rsqrt_fusion, f32[2048]{0:T(1024)S(1)} %copy-done.4, bf16[8,64,6144]{2,1,0:T(8,128)(2,1)} %copy-done.3, bf16[2048,6144]{1,0:T(8,128)(2,1)} %w_qkv.1), kind=kOutput, calls=%fused_computation.15 | convolution fusion | flops 12892239872 | bytes 37769216 | tf_op jit(solution)/shard_map/bse,de->bsd/dot_general | solution.py:577
  446.5 1.8 broadcast_select_fusion.1
  448.4 5.7 %fusion.13 = bf16[8,64,2048]{2,1,0:T(8,128)(2,1)} fusion(bf16[8,64,2048]{2,1,0:T(8,128)(2,1)S(1)} %copy-done, bf16[2048,2048]{1,0:T(8,128)(2,1)S(1)} %bitcast.21, bf16[8,64,1024]{2,1,0:T(8,128)(2,1)S(1)} %get-tuple-element.44, bf16[8,64,1024]{2,1,0:T(8,128)(2,1)S(1)} %get-tuple-element.43), kind=kOutput, calls=%fused_computation.16 | convolution fusion | flops 4302307328 | bytes 14680064 | tf_op jit(solution)/shard_map/bsh,hd->bsd/dot_general | solution.py:574
  454.1 0.5 collective-permute-start.5
  454.6 3.2 collective-permute-done.5
  457.8 1.5 collective-permute-start.6
  459.3 2.8 fusion.11
  462.1 0.8 collective-permute-done.6
  462.9 0.6 add.46
  463.5 13.4 %gw_end.1 = f32[2048,6144]{1,0:T(8,128)} custom-call(f32[2048,512]{1,0:T(8,128)} %collective-permute-done.10.refs_0_, f32[2048,512]{1,0:T(8,128)S(1)} %collective-permute-done.11.refs_1_, f32[2048,6144]{1,0:T(8,128)} %get-tuple-element.39.refs_2_), custom_call_target="tpu_custom_call", output_to_operand_aliasing={{}: (2, {})} | custom-call | tf_op jit(solution)/shard_map/gw_end/pallas_call | solution.py:521
  (45 shorter events, 3.2 us)
Async XLA Ops:
  289.3 28.6 %collective-permute-start.8 = (f32[1024,2048]{1,0:T(8,128)S(1)}, f32[1024,2048]{1,0:T(8,128)}, u32[]{:S(2)}, u32[]{:S(2)}) collective-permute-start(f32[1024,2048]{1,0:T(8,128)S(1)} %get-tuple-element.31), channel_id=1, source_target_pairs={{0,1},{1,0},{2,3},{3,2},{4,5},{5,4},{6,7},{7,6},{8,9},{9,8},{10,11... | collective-permute-start | bytes 25165832 | tf_op jit(solution)/shard_map/ppermute | solution.py:554
  317.4 58.4 %collective-permute-start.7 = (f32[2048,1024]{1,0:T(8,128)}, f32[2048,1024]{1,0:T(8,128)}, u32[]{:S(2)}, u32[]{:S(2)}) collective-permute-start(f32[2048,1024]{1,0:T(8,128)} %get-tuple-element.28), channel_id=1, source_target_pairs={{0,1},{1,0},{2,3},{3,2},{4,5},{5,4},{6,7},{7,6},{8,9},{9,8},{10,11... | collective-permute-start | bytes 25165832 | tf_op jit(solution)/shard_map/ppermute | solution.py:554
  347.3 10.3 %copy-start = (bf16[8,64,2048]{2,1,0:T(8,128)(2,1)S(1)}, bf16[8,64,2048]{2,1,0:T(8,128)(2,1)}, u32[]{:S(2)}) copy-start(bf16[8,64,2048]{2,1,0:T(8,128)(2,1)} %x_loc.1) | copy-start | bytes 6291460
  347.4 28.5 %collective-permute-start.9 = (f32[2048,1024]{1,0:T(8,128)}, f32[2048,1024]{1,0:T(8,128)}, u32[]{:S(2)}, u32[]{:S(2)}) collective-permute-start(f32[2048,1024]{1,0:T(8,128)} %get-tuple-element.34), channel_id=1, source_target_pairs={{0,1},{1,0},{2,3},{3,2},{4,5},{5,4},{6,7},{7,6},{8,9},{9,8},{10,11... | collective-permute-start | bytes 25165832 | tf_op jit(solution)/shard_map/ppermute | solution.py:554
  349.9 12.2 %collective-permute-start.1 = (bf16[8,64,1024]{2,1,0:T(8,128)(2,1)}, bf16[8,64,1024]{2,1,0:T(8,128)(2,1)}, u32[]{:S(2)}, u32[]{:S(2)}) collective-permute-start(bf16[8,64,1024]{2,1,0:T(8,128)(2,1)} %constant_dynamic-slice_fusion.2), channel_id=1, source_target_pairs={{0,1},{1,0},{2,3},{3,2},{4,5},{5,4},{6,7},{7,6},{8,9},{9,8},{10,11... | collective-permute-start | bytes 3145736 | tf_op jit(solution)/shard_map/ppermute | solution.py:551
  352.6 17.2 %collective-permute-start.3 = (bf16[8,64,1024]{2,1,0:T(8,128)(2,1)}, bf16[8,64,1024]{2,1,0:T(8,128)(2,1)S(1)}, u32[]{:S(2)}, u32[]{:S(2)}) collective-permute-start(bf16[8,64,1024]{2,1,0:T(8,128)(2,1)} %constant_dynamic-slice_fusion), channel_id=1, source_target_pairs={{0,1},{1,0},{2,3},{3,2},{4,5},{5,4},{6,7},{7,6},{8,9},{9,8},{10,11... | collective-permute-start | bytes 3145736 | tf_op jit(solution)/shard_map/ppermute | solution.py:551
  355.0 11.1 %collective-permute-start.2 = (bf16[8,64,1024]{2,1,0:T(8,128)(2,1)}, bf16[8,64,1024]{2,1,0:T(8,128)(2,1)}, u32[]{:S(2)}, u32[]{:S(2)}) collective-permute-start(bf16[8,64,1024]{2,1,0:T(8,128)(2,1)} %constant_dynamic-slice_fusion.1), channel_id=1, source_target_pairs={{0,1},{1,0},{2,3},{3,2},{4,5},{5,4},{6,7},{7,6},{8,9},{9,8},{10,11... | collective-permute-start | bytes 3145736 | tf_op jit(solution)/shard_map/ppermute | solution.py:551
  362.0 84.5 %collective-permute-start = (bf16[8,64,1024]{2,1,0:T(8,128)(2,1)}, bf16[8,64,1024]{2,1,0:T(8,128)(2,1)S(1)}, u32[]{:S(2)}, u32[]{:S(2)}) collective-permute-start(bf16[8,64,1024]{2,1,0:T(8,128)(2,1)} %constant_dynamic-slice_fusion.3), channel_id=1, source_target_pairs={{0,1},{1,0},{2,3},{3,2},{4,5},{5,4},{6,7},{7,6},{8,9},{9,8},{10,11... | collective-permute-start | bytes 3145736 | tf_op jit(solution)/shard_map/ppermute | solution.py:551
  363.9 11.9 %slice-start = ((s8[8388608]{0:T(1024)(128)(4,1)}), s8[4194304]{0:T(1024)(128)(4,1)S(1)}, s32[]{:S(2)}) async-start(s8[8388608]{0:T(1024)(128)(4,1)} %bitcast.15), calls=%async_computation | async-start | bytes 8388608
  367.7 8.1 %slice-start.1 = ((s8[8388608]{0:T(1024)(128)(4,1)}), s8[4194304]{0:T(1024)(128)(4,1)S(1)}, s32[]{:S(2)}) async-start(s8[8388608]{0:T(1024)(128)(4,1)} %bitcast.15), calls=%async_computation.1 | async-start | bytes 8388608
  373.1 2.7 copy-start.3
  404.5 59.1 %collective-permute-start.10 = (f32[2048,512]{1,0:T(8,128)}, f32[2048,512]{1,0:T(8,128)}, u32[]{:S(2)}, u32[]{:S(2)}) collective-permute-start(f32[2048,512]{1,0:T(8,128)} %get-tuple-element.36), channel_id=1, source_target_pairs={{0,1},{1,0},{2,3},{3,2},{4,5},{5,4},{6,7},{7,6},{8,9},{9,8},{10,11... | collective-permute-start | bytes 12582920 | tf_op jit(solution)/shard_map/ppermute | solution.py:554
  404.9 21.2 %copy-start.4 = (f32[2048]{0:T(1024)S(1)}, f32[2048]{0:T(1024)}, u32[]{:S(2)}) copy-start(f32[2048]{0:T(1024)} %param.10) | copy-start | bytes 24580
  425.7 22.6 %slice-start.2 = ((s8[8388608]{0:T(1024)(128)(4,1)}), s8[4194304]{0:T(1024)(128)(4,1)S(1)}, s32[]{:S(2)}) async-start(s8[8388608]{0:T(1024)(128)(4,1)} %bitcast.20), calls=%async_computation.2 | async-start | bytes 8388608
  425.7 22.6 %slice-start.3 = ((s8[8388608]{0:T(1024)(128)(4,1)}), s8[4194304]{0:T(1024)(128)(4,1)S(1)}, s32[]{:S(2)}) async-start(s8[8388608]{0:T(1024)(128)(4,1)} %bitcast.20), calls=%async_computation.3 | async-start | bytes 8388608
  425.7 37.8 %collective-permute-start.11 = (f32[2048,512]{1,0:T(8,128)}, f32[2048,512]{1,0:T(8,128)S(1)}, u32[]{:S(2)}, u32[]{:S(2)}) collective-permute-start(f32[2048,512]{1,0:T(8,128)} %get-tuple-element.38), channel_id=1, source_target_pairs={{0,1},{1,0},{2,3},{3,2},{4,5},{5,4},{6,7},{7,6},{8,9},{9,8},{10,11... | collective-permute-start | bytes 12582920 | tf_op jit(solution)/shard_map/ppermute | solution.py:554
  446.3 7.8 %collective-permute-start.4 = (f32[2048]{0:T(1024)S(1)}, f32[2048]{0:T(1024)S(1)}, u32[]{:S(2)}, u32[]{:S(2)}) collective-permute-start(f32[2048]{0:T(1024)S(1)} %get-tuple-element.41), channel_id=1, source_target_pairs={{0,1},{1,0},{2,3},{3,2},{4,5},{5,4},{6,7},{7,6},{8,9},{9,8},{10,11... | collective-permute-start | bytes 24584 | tf_op jit(solution)/shard_map/ppermute | solution.py:581
  448.3 11.0 %copy-start.1 = (bf16[8,64,2048]{2,1,0:T(8,128)(2,1)S(1)}, bf16[8,64,2048]{2,1,0:T(8,128)(2,1)}, u32[]{:S(2)}) copy-start(bf16[8,64,2048]{2,1,0:T(8,128)(2,1)} %gy_loc.1) | copy-start | bytes 6291460
  448.3 11.0 %copy-start.2 = (f32[8,64,2048]{2,1,0:T(8,128)S(1)}, f32[8,64,2048]{2,1,0:T(8,128)}, u32[]{:S(2)}) copy-start(f32[8,64,2048]{2,1,0:T(8,128)} %get-tuple-element.47) | copy-start | bytes 12582916
  454.1 3.7 collective-permute-start.5
  457.8 5.2 %collective-permute-start.6 = (f32[2048]{0:T(1024)S(1)}, f32[2048]{0:T(1024)S(1)}, u32[]{:S(2)}, u32[]{:S(2)}) collective-permute-start(f32[2048]{0:T(1024)S(1)} %add.45), channel_id=1, source_target_pairs={{0,4},{1,5},{2,6},{3,7},{4,0},{5,1},{6,2},{7,3},{8,12},{9,13},{10,... | collective-permute-start | bytes 24584 | tf_op jit(solution)/shard_map/ppermute | solution.py:581
